TPU v7x, 32 devices: a whole 2x2x4 slice. The times are simulated.
32 devices in a mesh: py: 4 (over y, x), pz: 8 (over z, core).
Axes of the slice: x: 2, y: 2, z: 4, core: 2. Of those that a mesh axis runs over, the one named last changes fastest.
Arguments:
- positions: float32 [3, 131072], P(None, ('py', 'pz')), may hold values from 0 to 512, as said below
- masses: float32 [131072], P(('py', 'pz')), may hold values from 16 to 160
Outputs:
- forces: float32 [3, 32, 64, 512], P(None, 'py', 'pz')
Inputs may be any that keep to these rules, and one draw needn't show every extreme that they name: `positions`: the particles come in blocks of 4096 columns; in the block numbered a 8 + b, row 0 lies in [a 8, (a + 1) * 8), row 1 in [b * 8, (b + 1) * 8), and row 2 in [0, 512).
All inputs are finite; a program needn't handle non-finite values.
Results may differ from a plain program's by a relative error of at most 0.0003.
Values sent between devices are 32-bit elements; how exact they have to be, the bound alone decides.
A program may use at most 64 MiB of HBM per device.

v0:
```python
import functools
import math

import jax
import jax.numpy as jnp
import ml_dtypes
import numpy as np
from jax import lax
from jax.experimental import pallas as pl
from jax.experimental.pallas import tpu as pltpu
from jax.sharding import PartitionSpec as P

MESH = pl.DeviceIdType.MESH
F32 = jnp.float32
BF16 = jnp.bfloat16
SMOOTHING_SQ = 0.25
CELL = 8
PAIR = 2 * CELL
GROUPS = 128 // PAIR


def parts(table, count):
    out = []
    for _ in range(count):
        out.append(table.astype(ml_dtypes.bfloat16))
        table = table - out[-1].astype(np.float64)
    return np.stack(out)


def tables(n_py, n_pz, nx, nf):
    ny, nz = CELL * n_py, CELL * n_pz
    kept = nx // 2
    phase = (np.outer(np.arange(kept), np.arange(nx)) % nx) * (2 * np.pi / nx)
    line = np.concatenate([np.cos(phase), -np.sin(phase)])
    phase = (np.outer(np.arange(ny), np.arange(ny)) % ny) * (2 * np.pi / ny)
    eye = np.eye(nf)
    rows = np.concatenate([np.kron(np.cos(phase), eye), np.kron(np.sin(phase), eye)], axis=1)
    phase = (np.outer(np.arange(nz), np.arange(nz)) % nz) * (2 * np.pi / nz)
    cos, sin = np.cos(phase), np.sin(phase)
    forward = np.zeros((n_pz, 2, CELL, 2, nz))
    forward[:, 0, :, 0] = cos.reshape(n_pz, CELL, nz)
    forward[:, 0, :, 1] = -sin.reshape(n_pz, CELL, nz)
    forward[:, 1, :, 0] = sin.reshape(n_pz, CELL, nz)
    forward[:, 1, :, 1] = cos.reshape(n_pz, CELL, nz)
    forward = forward.reshape(2 * nz, 2, nz)
    turned = np.stack([forward[:, 1], -forward[:, 0]], axis=1)
    forward = np.concatenate([forward.reshape(2 * nz, 2 * nz), turned.reshape(2 * nz, 2 * nz)], 1)
    inverse = np.zeros((2, nz, n_pz, 2, CELL))
    inverse[0, :, :, 0] = cos.reshape(nz, n_pz, CELL)
    inverse[0, :, :, 1] = sin.reshape(nz, n_pz, CELL)
    inverse[1, :, :, 0] = -sin.reshape(nz, n_pz, CELL)
    inverse[1, :, :, 1] = cos.reshape(nz, n_pz, CELL)
    inverse = inverse.reshape(2 * nz, n_pz, 2, CELL)
    turned = np.stack([-inverse[:, :, 1], inverse[:, :, 0]], axis=2)
    inverse = np.concatenate([inverse.reshape(2 * nz, 2 * nz), turned.reshape(2 * nz, 2 * nz)], 1)
    return parts(line, 3), parts(rows, 3), parts(forward, 2), parts(inverse, 3)


def split(x, count=2):
    out = []
    for i in range(count):
        out.append(x.astype(BF16))
        if i < count - 1:
            x = x - out[-1].astype(F32)
    return out


def dot_parts(left, right, dims=((1,), (0,))):
    count = len(left)
    total = None
    for order in reversed(range(count)):
        for i in range(order + 1):
            term = lax.dot_general(
                left[i], right[order - i], (dims, ((), ())), preferred_element_type=F32
            )
            total = term if total is None else total + term
    return total


def swap_groups(tiles):
    group = lax.broadcasted_iota(jnp.int32, tiles[0].shape, 1) // PAIR
    moved = []
    for step in range(GROUPS):
        mixed = tiles[step]
        for a in range(1, GROUPS):
            mixed = jnp.where(group == a, tiles[(a + step) % GROUPS], mixed)
        moved.append(pltpu.roll(mixed, step * PAIR, 1) if step else mixed)
    out = []
    for a in range(GROUPS):
        mixed = moved[(0 - a) % GROUPS]
        for g in range(1, GROUPS):
            mixed = jnp.where(group == g, moved[(g - a) % GROUPS], mixed)
        out.append(mixed)
    return out


def green_factor(rank, n_py, n_pz, nx, nf):
    ny, nz = CELL * n_py, CELL * n_pz
    shape = (ny * nf, 2 * nz)
    row = lax.broadcasted_iota(jnp.int32, shape, 0)
    col = lax.broadcasted_iota(jnp.int32, shape, 1)

    def square(wave, period):
        folded = jnp.minimum(wave, period - wave).astype(F32)
        return (folded * (2.0 * math.pi / period)) ** 2

    wave_x = rank * nf + row % nf
    total = square(row // nf, ny) + square(col % nz, nz) + square(wave_x, nx)
    safe = jnp.where(total > 0, total, 1.0)
    green = jnp.where(total > 0, -4.0 * math.pi * jnp.exp(-SMOOTHING_SQ * total) / safe, 0.0)
    return green * (jnp.where(wave_x > 0, 2.0, 1.0) * (1.0 / float(ny * nz * nx)))


def kernel(
    n_py, n_pz, nx, nf, chunk,
    pos_hbm, mass_hbm, line_hbm, rows_hbm, fwd_hbm, inv_hbm,
    out_ref,
    pos_ref, mass_ref, line, rows, fwd, inv, table_sem,
    acc, halo_out, halo_in, halo_send, halo_recv,
    send1, recv1, field, send2, recv2, waves,
    send_sem1, recv_sem1, send_sem2, recv_sem2,
    edge_out, edge_in, edge_send, edge_recv,
):
    n = n_py * n_pz
    my_y, my_z = lax.axis_index("py"), lax.axis_index("pz")
    rank = my_y * n_pz + my_z

    loads = [
        pltpu.make_async_copy(src, dst, table_sem.at[i])
        for i, (src, dst) in enumerate(
            [
                (pos_hbm, pos_ref),
                (mass_hbm, mass_ref),
                (line_hbm, line),
                (rows_hbm, rows),
                (fwd_hbm, fwd),
                (inv_hbm, inv),
            ]
        )
    ]
    for load in loads:
        load.start()

    def coords(step):
        peer = lax.rem(rank + step, n)
        return peer, (peer // n_pz, lax.rem(peer, n_pz))

    barrier = pltpu.get_barrier_semaphore()

    @pl.loop(1, n)
    def _(step):
        pl.semaphore_signal(barrier, inc=1, device_id=coords(step)[1], device_id_type=MESH)

    base_y = (my_y * CELL).astype(F32)
    base_z = (my_z * CELL).astype(F32)
    acc[...] = jnp.zeros_like(acc)
    cell = lax.broadcasted_iota(jnp.int32, (CELL, chunk), 0).astype(F32)
    x_index = lax.broadcasted_iota(jnp.int32, (nx, chunk), 0).astype(F32)

    for load in loads[:2]:
        load.wait()

    @pl.loop(0, pos_ref.shape[1] // chunk)
    def _(turn):
        span = pl.ds(pl.multiple_of(turn * chunk, chunk), chunk)
        along_y = pos_ref[0:1, span] - base_y
        along_z = pos_ref[1:2, span] - base_z
        along_x = pos_ref[2:3, span]
        mass = mass_ref[0:1, span]
        floor_x = jnp.floor(along_x)
        frac_x = along_x - floor_x
        one_hot = jnp.where(x_index == floor_x, 1.0, 0.0).astype(BF16)
        hat_y = jnp.maximum(1.0 - jnp.abs(along_y - cell), 0.0)
        hat_z = jnp.maximum(1.0 - jnp.abs(along_z - cell), 0.0)
        last_y = jnp.maximum(along_y - (CELL - 1.0), 0.0)
        last_z = jnp.maximum(along_z - (CELL - 1.0), 0.0)
        highs, lows = [], []
        for share in (mass * (1.0 - frac_x), mass * frac_x):
            scaled = hat_z * share
            tiles = [hat_y[a : a + 1] * scaled for a in range(CELL)]
            tiles.append(last_y * scaled)
            tiles.append(hat_y * (last_z * share))
            tiles.append(jnp.where(cell == 0.0, last_y * (last_z * share), 0.0))
            high, low = split(jnp.concatenate(tiles, axis=0))
            highs.append(high)
            lows.append(low)
        stacked = jnp.concatenate(highs + lows, axis=0)
        acc[...] += lax.dot_general(
            stacked, one_hot, (((1,), (1,)), ((), ())), preferred_element_type=F32
        )

    plane = (CELL + 3) * CELL
    lower = acc[0:plane] + acc[2 * plane : 3 * plane]
    upper = acc[plane : 2 * plane] + acc[3 * plane : 4 * plane]
    grid = lower + pltpu.roll(upper, 1, 1)
    for i in range(3):
        halo_out[i] = grid[(CELL + i) * CELL : (CELL + i + 1) * CELL]

    up_y, up_z = lax.rem(my_y + 1, n_py), lax.rem(my_z + 1, n_pz)
    down_y, down_z = lax.rem(my_y + n_py - 1, n_py), lax.rem(my_z + n_pz - 1, n_pz)
    green = green_factor(rank, n_py, n_pz, nx, nf)
    pl.semaphore_wait(barrier, n - 1)
    halos = [
        pltpu.make_async_remote_copy(
            src_ref=halo_out.at[i],
            dst_ref=halo_in.at[i],
            send_sem=halo_send.at[i],
            recv_sem=halo_recv.at[i],
            device_id=target,
            device_id_type=MESH,
        )
        for i, target in enumerate([(up_y, my_z), (my_y, up_z), (up_y, up_z)])
    ]
    for halo in halos:
        halo.start()
    for load in loads[2:]:
        load.wait()
    for halo in halos:
        halo.wait()

    first = lax.broadcasted_iota(jnp.int32, (CELL, nx), 0) == 0
    beside = halo_in[1]
    doubled = []
    for a in range(CELL):
        tile = grid[a * CELL : (a + 1) * CELL]
        tile = tile + jnp.where(first, beside[a : a + 1], 0.0)
        if a == 0:
            tile = tile + halo_in[0] + jnp.where(first, halo_in[2], 0.0)
        doubled += [tile, tile]
    density = split(jnp.concatenate(doubled, axis=0))
    kept = nx // 2
    both = dot_parts([line[0], line[1]], density, ((1,), (1,)))
    is_real = lax.broadcasted_iota(jnp.int32, (kept, 2 * CELL * CELL), 1) // CELL % 2 == 0
    spectrum = jnp.where(is_real, both[:kept], both[kept:])
    for r in range(n):
        send1[r] = spectrum[r * nf : (r + 1) * nf]

    def exchange(source, target, send_sem, recv_sem):
        @pl.loop(1, n)
        def _(step):
            mirrored = n - step
            other_y = lax.rem(mirrored, n_py) ^ my_y
            other_z = (mirrored // n_py) ^ my_z
            peer, where = other_y * n_pz + other_z, (other_y, other_z)
            pltpu.make_async_remote_copy(
                src_ref=source.at[peer],
                dst_ref=target.at[rank],
                send_sem=send_sem,
                recv_sem=recv_sem,
                device_id=where,
                device_id_type=MESH,
            ).start()

        target[rank] = source[rank]
        others = pl.ds(0, n - 1)
        pltpu.make_async_copy(source.at[others], source.at[others], send_sem).wait()
        pltpu.make_async_copy(target.at[others], target.at[others], recv_sem).wait()

    exchange(send1, recv1, send_sem1, recv_sem1)

    for ay in range(n_py):
        for t in range(n_pz // GROUPS):
            tiles = [recv1[ay * n_pz + t * GROUPS + g] for g in range(GROUPS)]
            for a, tile in enumerate(swap_groups(tiles)):
                start = (ay * CELL + a) * nf
                field[start : start + nf, t * 128 : (t + 1) * 128] = tile
    width = 2 * CELL * n_pz

    def plane_transform(values, table):
        count = table.shape[0]
        along = dot_parts(split(values, count), [table[i] for i in range(count)])
        joined = jnp.concatenate([along[:, :width], along[:, width:]], axis=0)
        return dot_parts([rows[i] for i in range(count)], split(joined, count))

    values = field[...]
    row = lax.broadcasted_iota(jnp.int32, values.shape, 0)
    col = lax.broadcasted_iota(jnp.int32, values.shape, 1)
    constant = (row % nf + rank * nf == 0) & (col // CELL % 2 == 0)
    mean = jnp.sum(jnp.where(constant, values, 0.0), axis=0, keepdims=True)
    mean = jnp.sum(mean, axis=1, keepdims=True) * (1.0 / (CELL * CELL * n))
    values = values - jnp.where(constant, mean, 0.0)
    solved = plane_transform(plane_transform(values, fwd) * green, inv)
    for ay in range(n_py):
        for t in range(n_pz // GROUPS):
            tiles = []
            for a in range(CELL):
                start = (ay * CELL + a) * nf
                tiles.append(solved[start : start + nf, t * 128 : (t + 1) * 128])
            for g, tile in enumerate(swap_groups(tiles)):
                send2[ay * n_pz + t * GROUPS + g] = tile

    exchange(send2, recv2, send_sem2, recv_sem2)

    for r in range(n):
        waves[r * nf : (r + 1) * nf] = recv2[r]
    columns = split(jnp.transpose(waves[...]), 3)
    cosines = dot_parts(columns, [line[i, :kept] for i in range(3)])
    sines = dot_parts(columns, [line[i, kept:] for i in range(3)])
    potential = [
        cosines[a * PAIR : a * PAIR + CELL] + sines[a * PAIR + CELL : (a + 1) * PAIR]
        for a in range(CELL)
    ]
    edge_out[0] = potential[CELL - 1]
    edge_out[1] = potential[0]
    edge_out[2] = jnp.concatenate([tile[CELL - 1 : CELL] for tile in potential], axis=0)
    edge_out[3] = jnp.concatenate([tile[0:1] for tile in potential], axis=0)
    edges = [
        pltpu.make_async_remote_copy(
            src_ref=edge_out.at[i],
            dst_ref=edge_in.at[i],
            send_sem=edge_send.at[i],
            recv_sem=edge_recv.at[i],
            device_id=target,
            device_id_type=MESH,
        )
        for i, target in enumerate(
            [(up_y, my_z), (down_y, my_z), (my_y, up_z), (my_y, down_z)]
        )
    ]
    for edge in edges:
        edge.start()
    for a, tile in enumerate(potential):
        out_ref[2, a] = (pltpu.roll(tile, 1, 1) - pltpu.roll(tile, nx - 1, 1)) * 0.5
    for edge in edges:
        edge.wait()
    before, after = edge_in[2], edge_in[3]
    lane_row = lax.broadcasted_iota(jnp.int32, (CELL, nx), 0)
    for a, tile in enumerate(potential):
        below = potential[a - 1] if a else edge_in[0]
        above = potential[a + 1] if a < CELL - 1 else edge_in[1]
        out_ref[0, a] = (below - above) * 0.5
        lower = jnp.where(lane_row == 0, before[a : a + 1], pltpu.roll(tile, 1, 0))
        upper = jnp.where(lane_row == CELL - 1, after[a : a + 1], pltpu.roll(tile, CELL - 1, 0))
        out_ref[1, a] = (lower - upper) * 0.5


def solution(mesh):
    n_py, n_pz = mesh.shape["py"], mesh.shape["pz"]
    n = n_py * n_pz
    nx = 512
    nf = nx // 2 // n
    ny, nz = CELL * n_py, CELL * n_pz
    consts = tables(n_py, n_pz, nx, nf)

    def shards(positions, masses):
        chunk = min(positions.shape[1], 1024)
        vmem = pl.BlockSpec(memory_space=pltpu.VMEM)
        hbm = pl.BlockSpec(memory_space=pltpu.HBM)
        plane = (CELL + 3) * CELL
        block = pltpu.VMEM((n, nf, 128), F32)
        dma = pltpu.SemaphoreType.DMA
        return pl.pallas_call(
            functools.partial(kernel, n_py, n_pz, nx, nf, chunk),
            out_shape=jax.ShapeDtypeStruct((3, CELL, CELL, nx), F32),
            in_specs=[hbm] * 6,
            out_specs=vmem,
            scratch_shapes=[
                pltpu.VMEM(positions.shape, F32),
                pltpu.VMEM((1, positions.shape[1]), F32),
                *[pltpu.VMEM(table.shape, BF16) for table in consts],
                dma((6,)),
                pltpu.VMEM((4 * plane, nx), F32),
                pltpu.VMEM((3, CELL, nx), F32),
                pltpu.VMEM((3, CELL, nx), F32),
                dma((3,)),
                dma((3,)),
                block,
                block,
                pltpu.VMEM((ny * nf, 2 * nz), F32),
                block,
                block,
                pltpu.VMEM((n * nf, 128), F32),
                dma, dma, dma, dma,
                pltpu.VMEM((4, CELL, nx), F32),
                pltpu.VMEM((4, CELL, nx), F32),
                dma((4,)),
                dma((4,)),
            ],
            compiler_params=pltpu.CompilerParams(
                collective_id=0, has_side_effects=True, vmem_limit_bytes=67_043_328
            ),
        )(positions, masses.reshape(1, -1), *[jnp.asarray(table) for table in consts])

    return jax.shard_map(
        shards,
        mesh=mesh,
        in_specs=(P(None, ("py", "pz")), P(("py", "pz"))),
        out_specs=P(None, "py", "pz", None),
        check_vma=False,
    )
```

profile of v0, /device:TPU:0, one launch (start us, length us, event | category | flops | bytes accessed | tf_op | source)
XLA Modules:
  0.0 30.8 jit_solution(10372470989601322585)
XLA Ops:
  0.0 29.0 %shard_map.64 = f32[3,8,8,512]{3,2,1,0:T(8,128)} custom-call(f32[3,4096]{1,0:T(4,128)} %pos_hbm.1, f32[1,4096]{1,0:T(1,128)} %bitcast.1, bf16[3,512,512]{2,1,0:T(8,128)(2,1)} %constant.8.clone.line_hbm, bf16[3,256,512]{2,1,0:T(8,128)(2,1)} %constant.9.clone.rows_hbm, bf16[2,128,256]{2,1,0:T(8,128)(2,1)} %constant.10.clone.fwd_hbm, ...), custom_call_target="tpu_custom_call" | custom-call | tf_op jit(solution)/shard_map/pallas_call | solution.py:352
  29.0 1.8 %copy.8 = f32[3,8,8,512]{3,2,1,0:T(8,128)} copy(f32[3,8,8,512]{3,2,1,0:T(8,128)} %shard_map.64) | data formatting | bytes 786432
where the time goes:
time: 31 us; the launch traced here: 30.8 us
  Pallas kernels  29 us (94%)
  local copies, waits for them, and re-layouts  1.77 us (6%)
    pallas_call x1, Pallas kernels, shards(): pl.pallas_call(functools.partial(kernel, n_py, n_pz, nx, nf, chunk), out_...  29 us
    unnamed x1, local copies, waits for them, and re-layouts  1.77 us

commit v1 on v0

--- a/solution.py
+++ b/solution.py
@@ -116,7 +116,7 @@
     pos_hbm, mass_hbm, line_hbm, rows_hbm, fwd_hbm, inv_hbm,
     out_ref,
     pos_ref, mass_ref, line, rows, fwd, inv, table_sem,
-    acc, halo_out, halo_in, halo_send, halo_recv,
+    hot, acc_halo, acc, halo_out, halo_in, halo_send, halo_recv,
     send1, recv1, field, send2, recv2, waves,
     send_sem1, recv_sem1, send_sem2, recv_sem2,
     edge_out, edge_in, edge_send, edge_recv,
@@ -142,8 +142,9 @@
         load.start()
 
     def coords(step):
-        peer = lax.rem(rank + step, n)
-        return peer, (peer // n_pz, lax.rem(peer, n_pz))
+        other_y = lax.rem(n - step, n_py) ^ my_y
+        other_z = ((n - step) // n_py) ^ my_z
+        return other_y * n_pz + other_z, (other_y, other_z)
 
     barrier = pltpu.get_barrier_semaphore()
 
@@ -154,14 +155,14 @@
     base_y = (my_y * CELL).astype(F32)
     base_z = (my_z * CELL).astype(F32)
     acc[...] = jnp.zeros_like(acc)
+    acc_halo[...] = jnp.zeros_like(acc_halo)
     cell = lax.broadcasted_iota(jnp.int32, (CELL, chunk), 0).astype(F32)
     x_index = lax.broadcasted_iota(jnp.int32, (nx, chunk), 0).astype(F32)
 
     for load in loads[:2]:
         load.wait()
 
-    @pl.loop(0, pos_ref.shape[1] // chunk)
-    def _(turn):
+    def weights(turn):
         span = pl.ds(pl.multiple_of(turn * chunk, chunk), chunk)
         along_y = pos_ref[0:1, span] - base_y
         along_z = pos_ref[1:2, span] - base_z
@@ -169,36 +170,49 @@
         mass = mass_ref[0:1, span]
         floor_x = jnp.floor(along_x)
         frac_x = along_x - floor_x
-        one_hot = jnp.where(x_index == floor_x, 1.0, 0.0).astype(BF16)
         hat_y = jnp.maximum(1.0 - jnp.abs(along_y - cell), 0.0)
         hat_z = jnp.maximum(1.0 - jnp.abs(along_z - cell), 0.0)
         last_y = jnp.maximum(along_y - (CELL - 1.0), 0.0)
         last_z = jnp.maximum(along_z - (CELL - 1.0), 0.0)
-        highs, lows = [], []
-        for share in (mass * (1.0 - frac_x), mass * frac_x):
-            scaled = hat_z * share
-            tiles = [hat_y[a : a + 1] * scaled for a in range(CELL)]
-            tiles.append(last_y * scaled)
-            tiles.append(hat_y * (last_z * share))
-            tiles.append(jnp.where(cell == 0.0, last_y * (last_z * share), 0.0))
-            high, low = split(jnp.concatenate(tiles, axis=0))
-            highs.append(high)
-            lows.append(low)
-        stacked = jnp.concatenate(highs + lows, axis=0)
-        acc[...] += lax.dot_general(
+        shares = (mass * (1.0 - frac_x), mass * frac_x)
+        return span, floor_x, hat_y, hat_z, last_y, last_z, shares
+
+    def deposited(tile_sets, one_hot):
+        pairs = [split(jnp.concatenate(tiles, axis=0)) for tiles in tile_sets]
+        stacked = jnp.concatenate([pair[i] for i in range(2) for pair in pairs], axis=0)
+        return lax.dot_general(
             stacked, one_hot, (((1,), (1,)), ((), ())), preferred_element_type=F32
         )
 
-    plane = (CELL + 3) * CELL
-    lower = acc[0:plane] + acc[2 * plane : 3 * plane]
-    upper = acc[plane : 2 * plane] + acc[3 * plane : 4 * plane]
-    grid = lower + pltpu.roll(upper, 1, 1)
+    def settled(sums):
+        plane = sums.shape[0] // 4
+        lower = sums[0:plane] + sums[2 * plane : 3 * plane]
+        upper = sums[plane : 2 * plane] + sums[3 * plane : 4 * plane]
+        return lower + pltpu.roll(upper, 1, 1)
+
+    turns = pos_ref.shape[1] // chunk
+
+    @pl.loop(0, turns)
+    def _(turn):
+        span, floor_x, hat_y, hat_z, last_y, last_z, shares = weights(turn)
+        one_hot = jnp.where(x_index == floor_x, 1.0, 0.0).astype(BF16)
+        hot[:, span] = one_hot
+        tile_sets = [
+            [
+                last_y * (hat_z * share),
+                hat_y * (last_z * share),
+                jnp.where(cell == 0.0, last_y * (last_z * share), 0.0),
+            ]
+            for share in shares
+        ]
+        acc_halo[...] += deposited(tile_sets, one_hot)
+
+    outer = settled(acc_halo[...])
     for i in range(3):
-        halo_out[i] = grid[(CELL + i) * CELL : (CELL + i + 1) * CELL]
+        halo_out[i] = outer[i * CELL : (i + 1) * CELL]
 
     up_y, up_z = lax.rem(my_y + 1, n_py), lax.rem(my_z + 1, n_pz)
     down_y, down_z = lax.rem(my_y + n_py - 1, n_py), lax.rem(my_z + n_pz - 1, n_pz)
-    green = green_factor(rank, n_py, n_pz, nx, nf)
     pl.semaphore_wait(barrier, n - 1)
     halos = [
         pltpu.make_async_remote_copy(
@@ -213,6 +227,18 @@
     ]
     for halo in halos:
         halo.start()
+
+    @pl.loop(0, turns)
+    def _(turn):
+        span, _, hat_y, hat_z, _, _, shares = weights(turn)
+        tile_sets = []
+        for share in shares:
+            scaled = hat_z * share
+            tile_sets.append([hat_y[a : a + 1] * scaled for a in range(CELL)])
+        acc[...] += deposited(tile_sets, hot[:, span])
+
+    grid = settled(acc[...])
+    green = green_factor(rank, n_py, n_pz, nx, nf)
     for load in loads[2:]:
         load.wait()
     for halo in halos:
@@ -238,10 +264,7 @@
     def exchange(source, target, send_sem, recv_sem):
         @pl.loop(1, n)
         def _(step):
-            mirrored = n - step
-            other_y = lax.rem(mirrored, n_py) ^ my_y
-            other_z = (mirrored // n_py) ^ my_z
-            peer, where = other_y * n_pz + other_z, (other_y, other_z)
+            peer, where = coords(step)
             pltpu.make_async_remote_copy(
                 src_ref=source.at[peer],
                 dst_ref=target.at[rank],
@@ -343,10 +366,9 @@
     consts = tables(n_py, n_pz, nx, nf)
 
     def shards(positions, masses):
-        chunk = min(positions.shape[1], 1024)
+        chunk = min(positions.shape[1], 2048)
         vmem = pl.BlockSpec(memory_space=pltpu.VMEM)
         hbm = pl.BlockSpec(memory_space=pltpu.HBM)
-        plane = (CELL + 3) * CELL
         block = pltpu.VMEM((n, nf, 128), F32)
         dma = pltpu.SemaphoreType.DMA
         return pl.pallas_call(
@@ -359,7 +381,9 @@
                 pltpu.VMEM((1, positions.shape[1]), F32),
                 *[pltpu.VMEM(table.shape, BF16) for table in consts],
                 dma((6,)),
-                pltpu.VMEM((4 * plane, nx), F32),
+                pltpu.VMEM((nx, positions.shape[1]), BF16),
+                pltpu.VMEM((4 * 3 * CELL, nx), F32),
+                pltpu.VMEM((4 * CELL * CELL, nx), F32),
                 pltpu.VMEM((3, CELL, nx), F32),
                 pltpu.VMEM((3, CELL, nx), F32),
                 dma((3,)),

time: 31 us -> 30.5 us (0.984)
  Pallas kernels: 29 us -> 28.5 us
    pallas_call x1, Pallas kernels: 29 us -> 28.5 us  [shards(): pl.pallas_call(functools.partial(kernel, n_py, n_pz, nx, nf, chunk), out_...]
where the time goes in v1:
time: 30.5 us; the launch traced here: 30.3 us
  Pallas kernels  28.5 us (93%)
  local copies, waits for them, and re-layouts  1.77 us (6%)
    pallas_call x1, Pallas kernels, shards(): pl.pallas_call(functools.partial(kernel, n_py, n_pz, nx, nf, chunk), out_...  28.5 us
    unnamed x1, local copies, waits for them, and re-layouts  1.77 us

profile of v1, /device:TPU:0, one launch (start us, length us, event | category | flops | bytes accessed | tf_op | source)
XLA Modules:
  0.0 30.3 jit_solution(3683883781473046811)
XLA Ops:
  0.0 28.5 %shard_map.64 = f32[3,8,8,512]{3,2,1,0:T(8,128)} custom-call(f32[3,4096]{1,0:T(4,128)} %pos_hbm.1, f32[1,4096]{1,0:T(1,128)} %bitcast.1, bf16[3,512,512]{2,1,0:T(8,128)(2,1)} %constant.8.clone.line_hbm, bf16[3,256,512]{2,1,0:T(8,128)(2,1)} %constant.9.clone.rows_hbm, bf16[2,128,256]{2,1,0:T(8,128)(2,1)} %constant.10.clone.fwd_hbm, ...), custom_call_target="tpu_custom_call" | custom-call | tf_op jit(solution)/shard_map/pallas_call | solution.py:374
  28.5 1.8 %copy.8 = f32[3,8,8,512]{3,2,1,0:T(8,128)} copy(f32[3,8,8,512]{3,2,1,0:T(8,128)} %shard_map.64) | data formatting | bytes 786432
